TPU v7x, 32 devices: a whole 2x2x4 slice. The times are simulated.
32 devices in a mesh: rep: 2 (over x), dp: 16 (over y, z, core).
Axes of the slice: x: 2, y: 2, z: 4, core: 2. Of those that a mesh axis runs over, the one named last changes fastest.
Arguments:
- a: bfloat16 [32, 4, 4096, 1536], P(('rep', 'dp')), parts along dimension 0
- g: bfloat16 [32, 4, 4096, 4224], P(('rep', 'dp')), parts along dimension 0
Outputs:
- output: bfloat16 [8, 1536, 4224], P('rep'), parts along dimension 0
There are 2 independent parts. A program takes and returns all parts, laid end to end along the dimension named above; each array names one.
All inputs are finite; a program needn't handle non-finite values.
Results may differ from a plain program's by a relative error of at most 0.012.
Values are sent between devices in bfloat16 or wider.
A program may use at most 2 GiB of HBM per device.

v0:
```python
import jax
import jax.numpy as jnp


def solution(mesh):
    groups = mesh.shape["rep"]

    def step(a, g):
        a, g = (t.reshape(groups, -1, *t.shape[1:]) for t in (a, g))
        sums = jnp.einsum("rsntd,rsntf->rndf", a, g, preferred_element_type=jnp.float32)
        return sums.astype(jnp.bfloat16).reshape(-1, *sums.shape[2:])

    return step
```

profile of v0, /device:TPU:0, one launch (start us, length us, event | category | flops | bytes accessed | tf_op | source)
XLA Modules:
  0.0 2375.9 jit_solution(18248609893714179336)
XLA Ops:
  0.0 248.9 %fusion.2 = f32[1,4,1536,4224]{3,2,1,0:T(8,128)} fusion(bf16[1,4,4096,4224]{3,2,1,0:T(8,128)(2,1)} %param.1, bf16[1,4,4096,1536]{3,2,1,0:T(8,128)(2,1)} %param), kind=kOutput, calls=%fused_computation.2 | convolution fusion | flops 212600881152 | bytes 292552704 | tf_op jit(solution)/rsntd,rsntf->rndf/dot_general | solution.py:10
  248.9 2127.0 %all-reduce.2 = bf16[1,4,1536,4224]{3,2,1,0:T(8,128)(2,1)} all-reduce(f32[1,4,1536,4224]{3,2,1,0:T(8,128)} %fusion.2), channel_id=1, replica_groups=[2,16]<=[32], use_global_device_ids=true, to_apply=%add.clone | all-reduce | flops 25952256 | bytes 155713536 | tf_op jit(solution)/rsntd,rsntf->rndf/dot_general | solution.py:10
where the time goes:
time: 2380 us
  blocking collectives  2130 us (89%)
  matrix products  249 us (10%)
    dot_general x1, blocking collectives, step(): jnp.einsum('rsntd,rsntf->rndf', a, g, preferred_element_type=jnp.float32)  2130 us
    dot_general x1, matrix products, step(): jnp.einsum('rsntd,rsntf->rndf', a, g, preferred_element_type=jnp.float32)  249 us

commit v1 on v0

v1 whole, which is shorter than its diff:
```python
import functools

import jax
import jax.numpy as jnp
from jax import lax
from jax.experimental import pallas as pl
from jax.experimental.pallas import tpu as pltpu
from jax.sharding import PartitionSpec as P

MESH = pl.DeviceIdType.MESH
NM, TOK, D, FF = 4, 4096, 1536, 4224
HALF = D // 2
TM, TN, UM = 256, 1408, 128
TILES, SLICES = HALF // TM, FF // TN
CHUNKS = NM * SLICES * TILES
UPC = TM // UM
U = CHUNKS * UPC
STEPS = 2 * CHUNKS
GSTEPS = 2 * TILES
GROUPS = NM * SLICES
L0, LT = 1, 2
TOP = 8
OB = 16
RC = 8
BR = 24
TOTAL = STEPS + L0 + LT * TOP + 1
assert UPC == 2


def tree(u, y, z):
    pos, period = u % 10, u // 10
    third = pos // 3
    kind_b = (pos % 3 == 2) | (pos == 9)
    k = jnp.where(kind_b, third, 1 + (third + period) % 2)
    q = jnp.where(kind_b, (third + period) % 2, pos % 3)
    at_q = y == q
    on_line = kind_b | at_q
    at_k = z == k
    far = jnp.maximum(k, 3 - k)
    side = jnp.where(z < k, z, jnp.where(z > k, 3 - z, far))
    root = at_q & at_k
    height = jnp.where(
        kind_b, side + root.astype(jnp.int32), jnp.where(at_q, 1 + side, 0)
    )
    top = far + 1
    depth = jnp.abs(z - k) + (1 - at_q.astype(jnp.int32))
    child = (
        at_q & (at_k | ~kind_b),
        on_line & (z <= k) & (z > 0),
        on_line & (z >= k) & (z < 3),
    )
    parent = (
        ~at_q & (at_k | ~kind_b),
        on_line & (z > k),
        on_line & (z < k),
    )
    return height, top + depth, root, child, parent


def kernel(
    a_ref, g_ref, out_ref, box_ref,
    abuf, gbuf, sibout, own, outbox, stage,
    a_sem, g_sem, sib_send, recv, load, up_send, down_send, res, sibres,
):
    rep = lax.axis_index("rep")
    me = lax.axis_index("dp")
    core, z, y = me % 2, (me // 2) % 4, me // 8
    sib = (rep, me + 1 - 2 * core)
    near = (
        (rep, me + 8 - 16 * y),
        (rep, jnp.where(z > 0, me - 2, me + 2)),
        (rep, jnp.where(z < 3, me + 2, me - 2)),
    )

    def a_load(i):
        c = i // 2
        n, t = c // (SLICES * TILES), c % TILES
        half = jnp.where(i % 2 == 0, 1 - core, core)
        cols = pl.ds(pl.multiple_of(half * HALF + t * TM, 128), TM)
        return pltpu.make_async_copy(
            a_ref.at[0, n, :, cols], abuf.at[i % 2], a_sem.at[i % 2]
        )

    def g_load(gi):
        cols = pl.ds(pl.multiple_of((gi % SLICES) * TN, 128), TN)
        return pltpu.make_async_copy(
            g_ref.at[0, gi // SLICES, :, cols], gbuf.at[gi % 2], g_sem.at[gi % 2]
        )

    def remote(src, dst, send, rcv, device):
        return pltpu.make_async_remote_copy(
            src_ref=src, dst_ref=dst, send_sem=send, recv_sem=rcv,
            device_id=device, device_id_type=MESH,
        )

    def place(u):
        c = u // UPC
        n, s, t = c // (SLICES * TILES), (c // TILES) % SLICES, c % TILES
        row = pl.multiple_of(core * HALF + t * TM + (u % UPC) * UM, UM)
        col = pl.multiple_of(s * TN, 128)
        return out_ref.at[n, pl.ds(row, UM), pl.ds(col, TN)]

    def sib_copy(c, h):
        return remote(
            sibout.at[c % 2, pl.ds(h * UM, UM)], box_ref.at[c * UPC + h],
            sib_send.at[c % 2, h], recv.at[0, c * UPC + h], sib,
        )

    def up_copy(u, d):
        s = (1, 3, 2)[d]
        return remote(
            outbox.at[u % OB], box_ref.at[s * U + u], up_send.at[u % OB, 0],
            recv.at[s, u], near[d],
        )

    def root_copy(u, d):
        return remote(
            outbox.at[u % OB], place(u), up_send.at[u % OB, d],
            res.at[u], near[d],
        )

    def root_sib(u):
        return remote(
            outbox.at[u % OB], place(u), up_send.at[u % OB, 3], sibres.at[u], sib
        )

    def root_local(u):
        return pltpu.make_async_copy(
            outbox.at[u % OB], place(u), up_send.at[u % OB, 4]
        )

    def down_copy(u, d):
        return remote(place(u), place(u), down_send.at[u % BR, d], res.at[u], near[d])

    def down_sib(u):
        return remote(place(u), place(u), down_send.at[u % BR, 3], sibres.at[u], sib)

    def up_done(u):
        _, _, root, child, parent = tree(u, y, z)
        for d in range(3):
            @pl.when(parent[d])
            def _(d=d):
                up_copy(u, d).wait_send()

            @pl.when(root & child[d])
            def _(d=d):
                root_copy(u, d).wait_send()

        @pl.when(root)
        def _():
            root_sib(u).wait_send()
            root_local(u).wait()

    def down_done(u):
        _, _, root, child, _ = tree(u, y, z)
        for d in range(3):
            @pl.when(~root & child[d])
            def _(d=d):
                down_copy(u, d).wait_send()

        @pl.when(~root)
        def _():
            down_sib(u).wait_send()

    def stage_load(tau, u, s, slot):
        return pltpu.make_async_copy(
            box_ref.at[s * U + u], stage.at[tau, slot], load.at[tau, slot]
        )

    def gather(i):
        def one(tau, _):
            u = i - L0 - LT * tau
            ok = (u >= 0) & (u < U)
            uu = jnp.clip(u, 0, U - 1)
            height, _, _, child, _ = tree(uu, y, z)

            @pl.when(ok & (height == tau))
            def _():
                remote(box_ref.at[uu], box_ref.at[uu], sib_send.at[0, 0],
                       recv.at[0, uu], sib).wait_recv()
                stage_load(tau, uu, 0, 0).start()
                slot = jnp.int32(1)
                for d in range(3):
                    @pl.when(child[d])
                    def _(d=d, slot=slot):
                        b = box_ref.at[(d + 1) * U + uu]
                        remote(b, b, sib_send.at[0, 0], recv.at[d + 1, uu], sib).wait_recv()
                        stage_load(tau, uu, d + 1, slot).start()

                    slot = slot + child[d].astype(jnp.int32)

            return 0

        lax.fori_loop(0, 5, one, 0)

    def combine(i):
        def one(tau, _):
            u = i - L0 - LT * tau
            ok = (u >= 0) & (u < U)
            uu = jnp.clip(u, 0, U - 1)
            height, _, root, child, parent = tree(uu, y, z)
            count = sum(c.astype(jnp.int32) for c in child)

            @pl.when(ok & (height == tau))
            def _():
                @pl.when(uu >= OB)
                def _():
                    up_done(jnp.maximum(uu - OB, 0))

                for m in range(4):
                    @pl.when(count == m)
                    def _(m=m):
                        for slot in range(m + 1):
                            stage_load(tau, uu, 0, slot).wait()

                        def rows(r, _):
                            here = pl.ds(pl.multiple_of(r * 16, 16), 16)
                            there = pl.ds(
                                pl.multiple_of((uu % UPC) * UM + r * 16, 16), 16
                            )
                            acc = own[(uu // UPC) % RC, there, :]
                            for slot in range(m + 1):
                                acc = acc + stage[tau, slot, here, :].astype(jnp.float32)
                            outbox[uu % OB, here, :] = acc.astype(jnp.bfloat16)
                            return 0

                        lax.fori_loop(0, UM // 16, rows, 0)

                for d in range(3):
                    @pl.when(parent[d])
                    def _(d=d):
                        up_copy(uu, d).start()

                    @pl.when(root & child[d])
                    def _(d=d):
                        root_copy(uu, d).start()

                @pl.when(root)
                def _():
                    root_sib(uu).start()
                    root_local(uu).start()

            return 0

        lax.fori_loop(0, 5, one, 0)

    def forward(i):
        def one(tau, _):
            u = i - L0 - LT * tau
            ok = (u >= 0) & (u < U)
            uu = jnp.clip(u, 0, U - 1)
            _, when, root, child, _ = tree(uu, y, z)

            @pl.when(ok & (when == tau))
            def _():
                @pl.when(uu >= BR)
                def _():
                    down_done(jnp.maximum(uu - BR, 0))

                @pl.when(~root)
                def _():
                    remote(place(uu), place(uu), sib_send.at[0, 0], res.at[uu], sib).wait_recv()
                    for d in range(3):
                        @pl.when(child[d])
                        def _(d=d):
                            down_copy(uu, d).start()

                    down_sib(uu).start()

            return 0

        lax.fori_loop(3, TOP + 1, one, 0)

    def matmul(i):
        @pl.when(i % GSTEPS == 0)
        def _():
            g_load(i // GSTEPS).wait()

            @pl.when(i // GSTEPS + 1 < GROUPS)
            def _():
                g_load(i // GSTEPS + 1).start()

        a_load(i).wait()

        @pl.when(i + 1 < STEPS)
        def _():
            a_load(i + 1).start()

        c = i // 2

        def dot():
            return lax.dot_general(
                abuf[i % 2], gbuf[(i // GSTEPS) % 2], (((0,), (0,)), ((), ())),
                preferred_element_type=jnp.float32,
            )

        @pl.when(i % 2 == 0)
        def _():
            @pl.when(c >= 2)
            def _():
                for h in range(UPC):
                    sib_copy(jnp.maximum(c - 2, 0), h).wait_send()

            sibout[c % 2] = dot().astype(jnp.bfloat16)
            for h in range(UPC):
                sib_copy(c, h).start()

        @pl.when(i % 2 == 1)
        def _():
            own[c % RC] = dot()

    a_load(0).start()
    g_load(0).start()
    barrier = pltpu.get_barrier_semaphore()
    pl.semaphore_signal(barrier, inc=1, device_id=sib, device_id_type=MESH)
    pl.semaphore_signal(barrier, inc=1, device_id=near[0], device_id_type=MESH)

    @pl.when(z > 0)
    def _():
        pl.semaphore_signal(barrier, inc=1, device_id=near[1], device_id_type=MESH)

    @pl.when(z < 3)
    def _():
        pl.semaphore_signal(barrier, inc=1, device_id=near[2], device_id_type=MESH)

    inner = (z > 0) & (z < 3)

    @pl.when(inner)
    def _():
        pl.semaphore_wait(barrier, 4)

    @pl.when(~inner)
    def _():
        pl.semaphore_wait(barrier, 3)

    def step(i, _):
        forward(i)
        gather(i)

        @pl.when(i < STEPS)
        def _():
            matmul(i)

        combine(i)
        return 0

    lax.fori_loop(0, TOTAL, step, 0)

    for c in range(CHUNKS - 2, CHUNKS):
        for h in range(UPC):
            sib_copy(c, h).wait_send()

    def end_up(u, _):
        up_done(u)
        return 0

    lax.fori_loop(U - OB, U, end_up, 0)

    def end_down(u, _):
        down_done(u)
        return 0

    lax.fori_loop(U - BR, U, end_down, 0)

    def end_sib(u, _):
        c = u // UPC
        n, s, t = c // (SLICES * TILES), (c // TILES) % SLICES, c % TILES
        row = pl.multiple_of((1 - core) * HALF + t * TM + (u % UPC) * UM, UM)
        b = out_ref.at[n, pl.ds(row, UM), pl.ds(pl.multiple_of(s * TN, 128), TN)]
        remote(b, b, sib_send.at[0, 0], sibres.at[u], sib).wait_recv()
        return 0

    lax.fori_loop(0, U, end_sib, 0)


def solution(mesh):
    def body(a, g):
        dma = pltpu.SemaphoreType.DMA
        out, _ = pl.pallas_call(
            kernel,
            out_shape=[
                jax.ShapeDtypeStruct((NM, D, FF), jnp.bfloat16),
                jax.ShapeDtypeStruct((4 * U, UM, TN), jnp.bfloat16),
            ],
            in_specs=[pl.BlockSpec(memory_space=pl.ANY)] * 2,
            out_specs=[pl.BlockSpec(memory_space=pl.ANY)] * 2,
            scratch_shapes=[
                pltpu.VMEM((2, TOK, TM), jnp.bfloat16),
                pltpu.VMEM((2, TOK, TN), jnp.bfloat16),
                pltpu.VMEM((2, TM, TN), jnp.bfloat16),
                pltpu.VMEM((RC, TM, TN), jnp.float32),
                pltpu.VMEM((OB, UM, TN), jnp.bfloat16),
                pltpu.VMEM((5, 4, UM, TN), jnp.bfloat16),
                dma((2,)),
                dma((2,)),
                dma((2, UPC)),
                dma((4, U)),
                dma((5, 4)),
                dma((OB, 5)),
                dma((BR, 4)),
                dma((U,)),
                dma((U,)),
            ],
            compiler_params=pltpu.CompilerParams(
                collective_id=0, has_side_effects=True, vmem_limit_bytes=63 * 2**20
            ),
            cost_estimate=pl.CostEstimate(
                flops=2 * NM * TOK * D * FF,
                bytes_accessed=2 * NM * (TOK * (D + FF) + D * FF),
                transcendentals=0,
            ),
        )(a, g)
        return out

    return jax.shard_map(
        body, mesh=mesh, in_specs=(P(("rep", "dp")), P(("rep", "dp"))),
        out_specs=P("rep"), check_vma=False,
    )
```

time: 2380 us -> 813 us (0.34)
  blocking collectives: 2130 us -> 0 us
  Pallas kernels: 0 us -> 778 us
  matrix products: 249 us -> 0 us
  local copies, waits for them, and re-layouts: 0 us -> 34.6 us
    dot_general x1 -> x0, blocking collectives: 2130 us -> none  [step(): jnp.einsum('rsntd,rsntf->rndf', a, g, preferred_element_type=jnp.float32)]
    pallas_call x0 -> x1, Pallas kernels: none -> 778 us  [body(): pl.pallas_call(kernel, out_shape=[jax.ShapeDtypeStruct((NM, D, FF), jnp.b...]
    dot_general x1 -> x0, matrix products: 249 us -> none  [step(): jnp.einsum('rsntd,rsntf->rndf', a, g, preferred_element_type=jnp.float32)]
    unnamed x0 -> x1, local copies, waits for them, and re-layouts: none -> 34.6 us
where the time goes in v1:
time: 813 us
  Pallas kernels  778 us (96%)
  local copies, waits for them, and re-layouts  34.6 us (4%)
    pallas_call x1, Pallas kernels, body(): pl.pallas_call(kernel, out_shape=[jax.ShapeDtypeStruct((NM, D, FF), jnp.b...  778 us
    unnamed x1, local copies, waits for them, and re-layouts  34.6 us

profile of v1, /device:TPU:0, one launch (start us, length us, event | category | flops | bytes accessed | tf_op | source)
XLA Modules:
  0.0 813.1 jit_solution(10490057505045827072)
XLA Ops:
  0.0 778.5 %shard_map.28 = (bf16[4,1536,4224]{2,1,0:T(8,128)(2,1)}, bf16[288,128,1408]{2,1,0:T(8,128)(2,1)}) custom-call(bf16[1,4,4096,1536]{3,2,1,0:T(8,128)(2,1)} %a_ref.1, bf16[1,4,4096,4224]{3,2,1,0:T(8,128)(2,1)} %g_ref.1), custom_call_target="tpu_custom_call" | custom-call | flops 212600881152 | bytes 240648192 | tf_op jit(solution)/shard_map/pallas_call | solution.py:379
  778.5 34.6 %copy.4 = bf16[4,1536,4224]{2,1,0:T(8,128)(2,1)} copy(bf16[4,1536,4224]{2,1,0:T(8,128)(2,1)} %get-tuple-element.6) | data formatting | bytes 103809024

commit v2 on v1

--- a/solution.py
+++ b/solution.py
@@ -18,21 +18,46 @@
 STEPS = 2 * CHUNKS
 GSTEPS = 2 * TILES
 GROUPS = NM * SLICES
-L0, LT = 1, 2
-TOP = 8
-OB = 16
-RC = 8
-BR = 24
-TOTAL = STEPS + L0 + LT * TOP + 1
-assert UPC == 2
+TREES = (
+    (False, 1, 1), (True, 1, 0), (False, 2, 1), (False, 2, 0), (False, 1, 0), (True, 2, 0), (False, 1, 0), (True, 1, 0),
+    (False, 2, 1), (False, 1, 1), (False, 2, 0), (False, 1, 1), (False, 1, 1), (False, 2, 1), (False, 1, 1), (False, 2, 0),
+    (False, 1, 0), (False, 2, 1), (True, 0, 1), (False, 2, 0), (False, 1, 1), (False, 1, 0), (False, 1, 0), (True, 2, 1),
+    (False, 1, 1), (False, 1, 1), (True, 3, 1), (True, 2, 1), (False, 1, 0), (False, 2, 1), (True, 3, 1), (True, 1, 0),
+    (True, 0, 1), (False, 1, 0), (False, 2, 1), (True, 1, 0), (False, 1, 1), (True, 1, 1), (True, 2, 1), (True, 2, 1),
+    (False, 1, 0), (True, 0, 0), (False, 1, 0), (True, 3, 1), (True, 1, 0), (False, 2, 0), (False, 1, 1), (True, 2, 1),
+    (False, 2, 1), (True, 1, 1), (False, 1, 1), (False, 1, 0), (False, 1, 1), (False, 2, 0), (False, 1, 1), (False, 1, 0),
+    (True, 3, 0), (False, 1, 0), (False, 2, 0), (False, 1, 1), (False, 2, 1), (False, 1, 1), (False, 1, 1), (False, 2, 0),
+    (False, 1, 0), (False, 1, 0), (False, 1, 0), (False, 1, 1), (True, 2, 1), (False, 2, 1), (False, 1, 0), (False, 1, 1),
+)
+LAG_UP = (1, 5, 9, 13, 17)
+LAG_DOWN = ((13, 19, 25, 31, 37), (17, 23, 29, 35, 41))
+OB = 18
+RC = 9
+BR = 30
+TOTAL = U + max(map(max, LAG_DOWN)) + 1
+assert UPC == 2 and OB > LAG_UP[4] - LAG_UP[0] and 2 * RC > LAG_UP[4]
+assert BR > max(map(max, LAG_DOWN)) - min(LAG_UP[3:])
+
+
+def pick(values, i):
+    out = jnp.int32(values[-1])
+    for j in reversed(range(len(values) - 1)):
+        out = jnp.where(i == j, values[j], out)
+    return out
+
+
+def bits(values, u):
+    words = [
+        sum(int(v) << j for j, v in enumerate(values[w : w + 24]))
+        for w in range(0, U, 24)
+    ]
+    return (pick(words, u // 24) >> (u % 24)) & 1
 
 
 def tree(u, y, z):
-    pos, period = u % 10, u // 10
-    third = pos // 3
-    kind_b = (pos % 3 == 2) | (pos == 9)
-    k = jnp.where(kind_b, third, 1 + (third + period) % 2)
-    q = jnp.where(kind_b, (third + period) % 2, pos % 3)
+    kind_b = bits([t[0] for t in TREES], u) == 1
+    k = bits([t[1] % 2 for t in TREES], u) + 2 * bits([t[1] // 2 for t in TREES], u)
+    q = bits([t[2] for t in TREES], u)
     at_q = y == q
     on_line = kind_b | at_q
     at_k = z == k
@@ -54,7 +79,7 @@
         on_line & (z > k),
         on_line & (z < k),
     )
-    return height, top + depth, root, child, parent
+    return height, top, depth, root, child, parent
 
 
 def kernel(
@@ -136,7 +161,7 @@
         return remote(place(u), place(u), down_send.at[u % BR, 3], sibres.at[u], sib)
 
     def up_done(u):
-        _, _, root, child, parent = tree(u, y, z)
+        _, _, _, root, child, parent = tree(u, y, z)
         for d in range(3):
             @pl.when(parent[d])
             def _(d=d):
@@ -152,7 +177,7 @@
             root_local(u).wait()
 
     def down_done(u):
-        _, _, root, child, _ = tree(u, y, z)
+        _, _, _, root, child, _ = tree(u, y, z)
         for d in range(3):
             @pl.when(~root & child[d])
             def _(d=d):
@@ -169,10 +194,10 @@
 
     def gather(i):
         def one(tau, _):
-            u = i - L0 - LT * tau
+            u = i - pick(LAG_UP, tau)
             ok = (u >= 0) & (u < U)
             uu = jnp.clip(u, 0, U - 1)
-            height, _, _, child, _ = tree(uu, y, z)
+            height, _, _, _, child, _ = tree(uu, y, z)
 
             @pl.when(ok & (height == tau))
             def _():
@@ -195,10 +220,10 @@
 
     def combine(i):
         def one(tau, _):
-            u = i - L0 - LT * tau
+            u = i - pick(LAG_UP, tau)
             ok = (u >= 0) & (u < U)
             uu = jnp.clip(u, 0, U - 1)
-            height, _, root, child, parent = tree(uu, y, z)
+            height, _, _, root, child, parent = tree(uu, y, z)
             count = sum(c.astype(jnp.int32) for c in child)
 
             @pl.when(ok & (height == tau))
@@ -246,12 +271,13 @@
 
     def forward(i):
         def one(tau, _):
-            u = i - L0 - LT * tau
+            up, down = 3 + tau // 5, tau % 5
+            u = i - pick(LAG_DOWN[0] + LAG_DOWN[1], tau)
             ok = (u >= 0) & (u < U)
             uu = jnp.clip(u, 0, U - 1)
-            _, when, root, child, _ = tree(uu, y, z)
-
-            @pl.when(ok & (when == tau))
+            _, top, depth, root, child, _ = tree(uu, y, z)
+
+            @pl.when(ok & (top == up) & (depth == down))
             def _():
                 @pl.when(uu >= BR)
                 def _():
@@ -269,7 +295,7 @@
 
             return 0
 
-        lax.fori_loop(3, TOP + 1, one, 0)
+        lax.fori_loop(0, 10, one, 0)
 
     def matmul(i):
         @pl.when(i % GSTEPS == 0)

time: 813 us -> 559 us (0.69)
  Pallas kernels: 778 us -> 524 us
    pallas_call x1, Pallas kernels: 778 us -> 524 us  [body(): pl.pallas_call(kernel, out_shape=[jax.ShapeDtypeStruct((NM, D, FF), jnp.b...]
where the time goes in v2:
time: 559 us
  Pallas kernels  524 us (94%)
  local copies, waits for them, and re-layouts  34.6 us (6%)
    pallas_call x1, Pallas kernels, body(): pl.pallas_call(kernel, out_shape=[jax.ShapeDtypeStruct((NM, D, FF), jnp.b...  524 us
    unnamed x1, local copies, waits for them, and re-layouts  34.6 us

profile of v2, /device:TPU:0, one launch (start us, length us, event | category | flops | bytes accessed | tf_op | source)
XLA Modules:
  0.0 558.6 jit_solution(6821232260731232981)
XLA Ops:
  0.0 524.0 %shard_map.28 = (bf16[4,1536,4224]{2,1,0:T(8,128)(2,1)}, bf16[288,128,1408]{2,1,0:T(8,128)(2,1)}) custom-call(bf16[1,4,4096,1536]{3,2,1,0:T(8,128)(2,1)} %a_ref.1, bf16[1,4,4096,4224]{3,2,1,0:T(8,128)(2,1)} %g_ref.1), custom_call_target="tpu_custom_call" | custom-call | flops 212600881152 | bytes 240648192 | tf_op jit(solution)/shard_map/pallas_call | solution.py:405
  524.0 34.6 %copy.4 = bf16[4,1536,4224]{2,1,0:T(8,128)(2,1)} copy(bf16[4,1536,4224]{2,1,0:T(8,128)(2,1)} %get-tuple-element.6) | data formatting | bytes 103809024
